TPU v7x, 32 devices: a whole 2x2x4 slice. The times are simulated.
32 devices in a mesh: group: 8 (over z, core), member: 4 (over y, x).
Axes of the slice: x: 2, y: 2, z: 4, core: 2. Of those that a mesh axis runs over, the one named last changes fastest.
Arguments:
- source: float32 [256, 128, 128], P('group', 'member'), may hold values from -5 to 8
- potential: float32 [256, 128, 128], P('group', 'member'), may hold values from -3 to 3
- refined: int32 [8, 4, 4], P('group', 'member'), may hold values 0 or 1
Outputs:
- smoothed: float32 [256, 128, 128], P('group', 'member')
- residual: float32 [256, 128, 128], P('group', 'member')
Inputs may be any that keep to these rules, and one draw needn't show every extreme that they name: 1 marks a refined box, 0 one that is not smoothed on the fine level.
All inputs are finite; a program needn't handle non-finite values. No bound on the sum of `refined` on one device may be relied on, other than what follows from the above.
Results may differ from a plain program's by a relative error of at most 0.000035.
Values sent between devices are 32-bit elements; how exact they have to be, the bound alone decides.
A program may use at most 128 MiB of HBM per device.

v0:
```python
import jax
import jax.numpy as jnp
from jax import lax
from jax.sharding import PartitionSpec as P

PRE = 2
POST = 2
COARSE = 2


def with_halo(cells, sides, width):
    for axis, dim in sides:
        count = lax.axis_size(axis)
        ends = count - 1
        head = lax.slice_in_dim(cells, 0, width, axis=dim)
        tail = lax.slice_in_dim(cells, cells.shape[dim] - width, cells.shape[dim], axis=dim)
        cells = jnp.concatenate(
            [
                lax.ppermute(tail, axis, [(i, (i + 1) % count) for i in range(ends)]),
                cells,
                lax.ppermute(head, axis, [((i + 1) % count, i) for i in range(ends)]),
            ],
            axis=dim,
        )
    return cells


def stencil_sum(padded):
    total = padded[2:, 1:-1, 1:-1] + padded[:-2, 1:-1, 1:-1]
    total = total + padded[1:-1, 2:, 1:-1] + padded[1:-1, :-2, 1:-1]
    return total + padded[1:-1, 1:-1, 2:] + padded[1:-1, 1:-1, :-2]


def expand(values_in, factor):
    size_a, size_b, size_c = values_in.shape
    wide = jnp.broadcast_to(
        values_in[:, None, :, None, :, None], (size_a, factor, size_b, factor, size_c, factor)
    )
    return wide.reshape(size_a * factor, size_b * factor, size_c * factor)


def parity_at(shape, offset_x, offset_y):
    along_x = lax.broadcasted_iota(jnp.int32, shape, 0) + offset_x
    along_y = lax.broadcasted_iota(jnp.int32, shape, 1) + offset_y
    along_z = lax.broadcasted_iota(jnp.int32, shape, 2)
    return (along_x + along_y + along_z) % 2


def fine_padded(grid_field):
    padded = with_halo(grid_field, (("group", 0), ("member", 1)), 1)
    return jnp.pad(padded, ((0, 0), (0, 0), (1, 1)))


def slab_padded(grid_field):
    padded = with_halo(grid_field, (("group", 0),), 1)
    return jnp.pad(padded, ((0, 0), (1, 1), (1, 1)))


def red_black(grid_field, right_side, active, parity, padder):
    for colour in (0, 1):
        update = (right_side + stencil_sum(padder(grid_field))) / 6.0
        grid_field = jnp.where((parity == colour) & active, update, grid_field)
    return grid_field


def wide_sweeps(grid_field, right_side, active_flags, offset_x, offset_y, count):
    depth = 2 * count
    stacked = jnp.stack([grid_field, right_side, active_flags])
    wide = with_halo(stacked, (("group", 1), ("member", 2)), depth)
    field_wide = wide[0]
    right_wide = wide[1]
    mask_wide = wide[2] > 0.5
    parity_wide = parity_at(field_wide.shape, offset_x - depth, offset_y - depth)
    for _ in range(count):
        for colour in (0, 1):
            update = (right_wide + stencil_sum(jnp.pad(field_wide, 1))) / 6.0
            field_wide = jnp.where((parity_wide == colour) & mask_wide, update, field_wide)
    return field_wide[depth:-depth, depth:-depth, :]


def per_device(source, potential, refined):
    cells_x, cells_y, cells_z = source.shape
    groups = lax.axis_size("group")
    members = lax.axis_size("member")
    group_at = lax.axis_index("group")
    member_at = lax.axis_index("member")
    total_cells = cells_x * cells_y * cells_z * groups * members
    density_mean = lax.psum(jnp.sum(source), ("group", "member")) / total_cells
    contrast = source - density_mean
    active = expand(refined == 1, cells_x)
    active_flags = active.astype(jnp.float32)
    phi = potential
    phi = wide_sweeps(phi, contrast, active_flags, group_at * cells_x, member_at * cells_y, PRE)
    fine_residual = contrast - (6.0 * phi - stencil_sum(fine_padded(phi)))
    half_x, half_y, half_z = (cells_x // 2, cells_y // 2, cells_z // 2)
    coarse_source = fine_residual.reshape(half_x, 2, half_y, 2, half_z, 2).sum(axis=(1, 3, 5)) * 0.5
    reach = 2 * COARSE
    widened = with_halo(coarse_source, (("member", 1),), reach)
    slab_parity = parity_at(widened.shape, group_at * half_x, member_at * half_y - reach)
    global_y = lax.broadcasted_iota(jnp.int32, widened.shape, 1) + member_at * half_y - reach
    inside = (global_y >= 0) & (global_y < half_y * members)
    correction = jnp.zeros(widened.shape, jnp.float32)
    for _ in range(COARSE):
        correction = red_black(correction, widened, inside, slab_parity, slab_padded)
    correction = correction[:, reach : reach + half_y, :]
    phi = phi + expand(correction, 2)
    phi = wide_sweeps(phi, contrast, active_flags, group_at * cells_x, member_at * cells_y, POST)
    residual = contrast - (6.0 * phi - stencil_sum(fine_padded(phi)))
    return (phi, residual)


def solution(mesh):
    return jax.shard_map(
        per_device,
        mesh=mesh,
        in_specs=(
            P("group", "member", None),
            P("group", "member", None),
            P("group", "member", None),
        ),
        out_specs=(P("group", "member", None), P("group", "member", None)),
        check_vma=False,
    )
```

profile of v0, /device:TPU:28, one launch (start us, length us, event | category | flops | bytes accessed | tf_op | source)
XLA Modules:
  0.0 255.3 jit_solution(6025978741319817130)
XLA Ops:
  0.6 1.8 reduce_sum.18
  2.5 40.2 %psum.7 = f32[]{:T(128)} all-reduce(f32[]{:T(128)} %reduce_sum.18), channel_id=1, replica_groups=mesh['group'=8,'member'=4] {'group','member'}, use_global_device_ids=true, to_apply=%region_1.0 | all-reduce | flops 1 | bytes 8 | tf_op jit(solution)/shard_map/psum | solution.py:88
  43.4 1.1 subtract_bitcast_fusion
  44.4 0.7 fusion.118
  45.5 1.9 collective-permute-start
  47.4 3.6 %collective-permute-start.1 = (f32[3,4,32,128]{3,2,1,0:T(8,128)S(1)}, f32[3,4,32,128]{3,2,1,0:T(8,128)S(1)}, u32[]{:S(2)}, u32[]{:S(2)}) collective-permute-start(f32[3,4,32,128]{3,2,1,0:T(8,128)S(1)} %get-tuple-element.13), channel_id=1, source_target_pairs={{4,0},{8,4},{12,8},{16,12},{20,16},{24,20},{28,24},{5,1},{9,5},{13... | collective-permute-start | bytes 589832 | tf_op jit(solution)/shard_map/ppermute | solution.py:21
  51.1 1.4 collective-permute-done
  52.5 1.8 collective-permute-done.1
  54.5 2.5 collective-permute-start.2
  57.0 4.3 %collective-permute-start.3 = (f32[3,40,4,128]{3,2,1,0:T(4,128)S(1)}, f32[3,40,4,128]{3,2,1,0:T(4,128)S(1)}, u32[]{:S(2)}, u32[]{:S(2)}) collective-permute-start(f32[3,40,4,128]{3,2,1,0:T(4,128)S(1)} %get-tuple-element.9), channel_id=1, source_target_pairs={{1,0},{2,1},{3,2},{5,4},{6,5},{7,6},{9,8},{10,9},{11,10},{13,12},{... | collective-permute-start | bytes 737288 | tf_op jit(solution)/shard_map/ppermute | solution.py:21
  61.3 3.3 %collective-permute-start.10 = (f32[1,24,64]{2,1,0:T(8,128)S(1)}, f32[1,24,64]{2,1,0:T(8,128)S(1)}, u32[]{:S(2)}, u32[]{:S(2)}) collective-permute-start(f32[1,24,64]{2,1,0:T(8,128)S(1)} %broadcast.116), channel_id=1, source_target_pairs={{4,0},{8,4},{12,8},{16,12},{20,16},{24,20},{28,24},{5,1},{9,5},{13... | collective-permute-start | bytes 18440 | tf_op jit(solution)/shard_map/ppermute | solution.py:21
  64.5 1.9 collective-permute-start.11
  66.5 0.4 fusion.3
  67.0 1.0 fusion.21
  68.0 0.9 fusion.29
  68.9 0.9 fusion.37
  69.8 0.9 fusion.45
  70.8 4.9 %collective-permute-start.4 = (f32[1,32,128]{2,1,0:T(8,128)S(1)}, f32[1,32,128]{2,1,0:T(8,128)S(1)}, u32[]{:S(2)}, u32[]{:S(2)}) collective-permute-start(f32[1,32,128]{2,1,0:T(8,128)S(1)} %get-tuple-element.17), channel_id=1, source_target_pairs={{4,0},{8,4},{12,8},{16,12},{20,16},{24,20},{28,24},{5,1},{9,5},{13... | collective-permute-start | bytes 49160 | tf_op jit(solution)/shard_map/ppermute | solution.py:21
  75.7 1.9 collective-permute-start.5
  77.7 3.0 %collective-permute-done.5 = f32[1,32,128]{2,1,0:T(8,128)S(1)} collective-permute-done((f32[1,32,128]{2,1,0:T(8,128)S(1)}, f32[1,32,128]{2,1,0:T(8,128)S(1)}, u32[]{:S(2)}, u32[]{:S(2)}) %collective-permute-start.5) | collective-permute-done | bytes 16416 | tf_op jit(solution)/shard_map/ppermute | solution.py:19
  80.8 5.3 %collective-permute-start.6 = (f32[34,1,128]{2,1,0:T(1,128)S(1)}, f32[34,1,128]{2,1,0:T(1,128)S(1)}, u32[]{:S(2)}, u32[]{:S(2)}) collective-permute-start(f32[34,1,128]{2,1,0:T(1,128)S(1)} %get-tuple-element.21), channel_id=1, source_target_pairs={{1,0},{2,1},{3,2},{5,4},{6,5},{7,6},{9,8},{10,9},{11,10},{13,12},{... | collective-permute-start | bytes 52232 | tf_op jit(solution)/shard_map/ppermute | solution.py:21
  86.0 1.9 collective-permute-start.7
  88.0 4.6 %collective-permute-done.7 = f32[34,1,128]{2,1,0:T(1,128)S(1)} collective-permute-done((f32[34,1,128]{2,1,0:T(1,128)S(1)}, f32[34,1,128]{2,1,0:T(1,128)S(1)}, u32[]{:S(2)}, u32[]{:S(2)}) %collective-permute-start.7) | collective-permute-done | bytes 17440 | tf_op jit(solution)/shard_map/ppermute | solution.py:19
  92.6 0.6 select_maximum_fusion.4
  93.2 0.4 fusion.88
  93.6 34.9 %reshape.24 = f32[16,2,16,2,64,2]{5,4,3,2,1,0:T(8,128)} reshape(f32[32,32,128]{2,1,0:T(8,128)S(1)} %fusion.88) | data formatting | bytes 1048576 | tf_op jit(solution)/shard_map/reshape | solution.py:96
  128.5 12.2 %reduce_sum.19 = f32[16,16,64]{2,1,0:T(8,128)S(1)} reduce(f32[16,2,16,2,64,2]{5,4,3,2,1,0:T(8,128)} %reshape.24, f32[]{:T(128)} %constant.75.clone.1), dimensions={1,3,5}, to_apply=%region_2.3 | reduce | flops 114688 | bytes 589828 | tf_op jit(solution)/shard_map/reduce_sum | solution.py:96
  140.7 1.9 collective-permute-start.8
  142.6 4.8 %collective-permute-start.9 = (f32[16,4,64]{2,1,0:T(4,128)S(1)}, f32[16,4,64]{2,1,0:T(4,128)S(1)}, u32[]{:S(2)}, u32[]{:S(2)}) collective-permute-start(f32[16,4,64]{2,1,0:T(4,128)S(1)} %get-tuple-element.35), channel_id=1, source_target_pairs={{1,0},{2,1},{3,2},{5,4},{6,5},{7,6},{9,8},{10,9},{11,10},{13,12},{... | collective-permute-start | bytes 49160 | tf_op jit(solution)/shard_map/ppermute | solution.py:21
  147.7 1.4 collective-permute-done.9
  149.0 0.3 pad_maximum_fusion.34
  149.3 1.9 collective-permute-start.12
  151.3 2.4 collective-permute-start.13
  153.7 2.6 %collective-permute-done.13 = f32[1,24,64]{2,1,0:T(8,128)S(1)} collective-permute-done((f32[1,24,64]{2,1,0:T(8,128)S(1)}, f32[1,24,64]{2,1,0:T(8,128)S(1)}, u32[]{:S(2)}, u32[]{:S(2)}) %collective-permute-start.13) | collective-permute-done | bytes 6176 | tf_op jit(solution)/shard_map/ppermute | solution.py:19
  156.4 0.3 fusion.115
  156.8 1.9 collective-permute-start.14
  158.7 2.4 collective-permute-start.15
  161.1 2.6 %collective-permute-done.15 = f32[1,24,64]{2,1,0:T(8,128)S(1)} collective-permute-done((f32[1,24,64]{2,1,0:T(8,128)S(1)}, f32[1,24,64]{2,1,0:T(8,128)S(1)}, u32[]{:S(2)}, u32[]{:S(2)}) %collective-permute-start.15) | collective-permute-done | bytes 6176 | tf_op jit(solution)/shard_map/ppermute | solution.py:19
  163.8 0.3 fusion.111
  164.2 1.9 collective-permute-start.16
  166.1 2.6 %collective-permute-start.17 = (f32[1,24,64]{2,1,0:T(8,128)S(1)}, f32[1,24,64]{2,1,0:T(8,128)S(1)}, u32[]{:S(2)}, u32[]{:S(2)}) collective-permute-start(f32[1,24,64]{2,1,0:T(8,128)S(1)} %get-tuple-element.26), channel_id=1, source_target_pairs={{0,4},{4,8},{8,12},{12,16},{16,20},{20,24},{24,28},{1,5},{5,9},{9,... | collective-permute-start | bytes 18440 | tf_op jit(solution)/shard_map/ppermute | solution.py:19
  168.9 2.2 collective-permute-done.17
  171.6 11.4 %broadcast_in_dim.20 = f32[16,2,16,2,64,2]{5,4,3,2,1,0:T(8,128)} broadcast(f32[16,16,64]{2,1,0:T(8,128)S(1)} %slice_select_fusion), dimensions={0,2,4} | broadcast | bytes 589824 | tf_op jit(solution)/shard_map/broadcast_in_dim | solution.py:36
  183.0 24.0 %reshape.25 = f32[32,32,128]{2,1,0:T(8,128)S(1)} reshape(f32[16,2,16,2,64,2]{5,4,3,2,1,0:T(8,128)} %broadcast_in_dim.20) | data formatting | bytes 1048576 | tf_op jit(solution)/shard_map/reshape | solution.py:39
  207.2 1.9 collective-permute-start.18
  209.2 3.6 %collective-permute-start.19 = (f32[3,4,32,128]{3,2,1,0:T(8,128)S(1)}, f32[3,4,32,128]{3,2,1,0:T(8,128)S(1)}, u32[]{:S(2)}, u32[]{:S(2)}) collective-permute-start(f32[3,4,32,128]{3,2,1,0:T(8,128)S(1)} %get-tuple-element.11), channel_id=1, source_target_pairs={{4,0},{8,4},{12,8},{16,12},{20,16},{24,20},{28,24},{5,1},{9,5},{13... | collective-permute-start | bytes 589832 | tf_op jit(solution)/shard_map/ppermute | solution.py:21
  212.8 1.4 collective-permute-done.18
  214.2 1.8 collective-permute-done.19
  216.3 1.9 collective-permute-start.20
  218.2 5.1 %collective-permute-start.21 = (f32[3,40,4,128]{3,2,1,0:T(4,128)S(1)}, f32[3,40,4,128]{3,2,1,0:T(4,128)S(1)}, u32[]{:S(2)}, u32[]{:S(2)}) collective-permute-start(f32[3,40,4,128]{3,2,1,0:T(4,128)S(1)} %get-tuple-element.7), channel_id=1, source_target_pairs={{1,0},{2,1},{3,2},{5,4},{6,5},{7,6},{9,8},{10,9},{11,10},{13,12},{... | collective-permute-start | bytes 737288 | tf_op jit(solution)/shard_map/ppermute | solution.py:21
  223.3 4.2 %collective-permute-done.20 = f32[3,40,4,128]{3,2,1,0:T(4,128)S(1)} collective-permute-done((f32[3,40,4,128]{3,2,1,0:T(4,128)S(1)}, f32[3,40,4,128]{3,2,1,0:T(4,128)S(1)}, u32[]{:S(2)}, u32[]{:S(2)}) %collective-permute-start.20) | collective-permute-done | bytes 245792 | tf_op jit(solution)/shard_map/ppermute | solution.py:19
  227.5 0.4 fusion.7
  228.0 1.0 fusion.53
  229.1 1.0 fusion.61
  230.1 1.0 fusion.69
  231.0 0.9 fusion.77
  232.0 4.7 %collective-permute-start.22 = (f32[1,32,128]{2,1,0:T(8,128)S(1)}, f32[1,32,128]{2,1,0:T(8,128)S(1)}, u32[]{:S(2)}, u32[]{:S(2)}) collective-permute-start(f32[1,32,128]{2,1,0:T(8,128)S(1)} %get-tuple-element.15), channel_id=1, source_target_pairs={{4,0},{8,4},{12,8},{16,12},{20,16},{24,20},{28,24},{5,1},{9,5},{13... | collective-permute-start | bytes 49160 | tf_op jit(solution)/shard_map/ppermute | solution.py:21
  236.7 1.9 collective-permute-start.23
  238.7 3.0 %collective-permute-done.23 = f32[1,32,128]{2,1,0:T(8,128)S(1)} collective-permute-done((f32[1,32,128]{2,1,0:T(8,128)S(1)}, f32[1,32,128]{2,1,0:T(8,128)S(1)}, u32[]{:S(2)}, u32[]{:S(2)}) %collective-permute-start.23) | collective-permute-done | bytes 16416 | tf_op jit(solution)/shard_map/ppermute | solution.py:19
  241.8 5.1 %collective-permute-start.24 = (f32[34,1,128]{2,1,0:T(1,128)S(1)}, f32[34,1,128]{2,1,0:T(1,128)S(1)}, u32[]{:S(2)}, u32[]{:S(2)}) collective-permute-start(f32[34,1,128]{2,1,0:T(1,128)S(1)} %get-tuple-element.19), channel_id=1, source_target_pairs={{1,0},{2,1},{3,2},{5,4},{6,5},{7,6},{9,8},{10,9},{11,10},{13,12},{... | collective-permute-start | bytes 52232 | tf_op jit(solution)/shard_map/ppermute | solution.py:21
  246.9 1.9 collective-permute-start.25
  248.9 4.6 %collective-permute-done.25 = f32[34,1,128]{2,1,0:T(1,128)S(1)} collective-permute-done((f32[34,1,128]{2,1,0:T(1,128)S(1)}, f32[34,1,128]{2,1,0:T(1,128)S(1)}, u32[]{:S(2)}, u32[]{:S(2)}) %collective-permute-start.25) | collective-permute-done | bytes 17440 | tf_op jit(solution)/shard_map/ppermute | solution.py:19
  253.5 0.6 select_maximum_fusion
  254.1 1.2 fusion.83
  (57 shorter events, 2.6 us)
Async XLA Ops:
  0.6 44.7 %copy-start.2 = (f32[32,32,128]{2,1,0:T(8,128)S(1)}, f32[32,32,128]{2,1,0:T(8,128)}, u32[]{:S(2)}) copy-start(f32[32,32,128]{2,1,0:T(8,128)} %param.4) | copy-start | bytes 1572868
  45.5 7.0 %collective-permute-start = (f32[3,4,32,128]{3,2,1,0:T(8,128)S(1)}, f32[3,4,32,128]{3,2,1,0:T(8,128)S(1)}, u32[]{:S(2)}, u32[]{:S(2)}) collective-permute-start(f32[3,4,32,128]{3,2,1,0:T(8,128)S(1)} %get-tuple-element.12), channel_id=1, source_target_pairs={{0,4},{4,8},{8,12},{12,16},{16,20},{20,24},{24,28},{1,5},{5,9},{9,... | collective-permute-start | bytes 589832 | tf_op jit(solution)/shard_map/ppermute | solution.py:19
  47.4 6.8 %collective-permute-start.1 = (f32[3,4,32,128]{3,2,1,0:T(8,128)S(1)}, f32[3,4,32,128]{3,2,1,0:T(8,128)S(1)}, u32[]{:S(2)}, u32[]{:S(2)}) collective-permute-start(f32[3,4,32,128]{3,2,1,0:T(8,128)S(1)} %get-tuple-element.13), channel_id=1, source_target_pairs={{4,0},{8,4},{12,8},{16,12},{20,16},{24,20},{28,24},{5,1},{9,5},{13... | collective-permute-start | bytes 589832 | tf_op jit(solution)/shard_map/ppermute | solution.py:21
  54.5 12.0 %collective-permute-start.2 = (f32[3,40,4,128]{3,2,1,0:T(4,128)S(1)}, f32[3,40,4,128]{3,2,1,0:T(4,128)S(1)}, u32[]{:S(2)}, u32[]{:S(2)}) collective-permute-start(f32[3,40,4,128]{3,2,1,0:T(4,128)S(1)} %get-tuple-element.8), channel_id=1, source_target_pairs={{0,1},{1,2},{2,3},{4,5},{5,6},{6,7},{8,9},{9,10},{10,11},{12,13},{... | collective-permute-start | bytes 737288 | tf_op jit(solution)/shard_map/ppermute | solution.py:19
  57.0 9.5 %collective-permute-start.3 = (f32[3,40,4,128]{3,2,1,0:T(4,128)S(1)}, f32[3,40,4,128]{3,2,1,0:T(4,128)S(1)}, u32[]{:S(2)}, u32[]{:S(2)}) collective-permute-start(f32[3,40,4,128]{3,2,1,0:T(4,128)S(1)} %get-tuple-element.9), channel_id=1, source_target_pairs={{1,0},{2,1},{3,2},{5,4},{6,5},{7,6},{9,8},{10,9},{11,10},{13,12},{... | collective-permute-start | bytes 737288 | tf_op jit(solution)/shard_map/ppermute | solution.py:21
  61.3 86.2 %collective-permute-start.10 = (f32[1,24,64]{2,1,0:T(8,128)S(1)}, f32[1,24,64]{2,1,0:T(8,128)S(1)}, u32[]{:S(2)}, u32[]{:S(2)}) collective-permute-start(f32[1,24,64]{2,1,0:T(8,128)S(1)} %broadcast.116), channel_id=1, source_target_pairs={{4,0},{8,4},{12,8},{16,12},{20,16},{24,20},{28,24},{5,1},{9,5},{13... | collective-permute-start | bytes 18440 | tf_op jit(solution)/shard_map/ppermute | solution.py:21
  64.5 83.0 %collective-permute-start.11 = (f32[1,24,64]{2,1,0:T(8,128)S(1)}, f32[1,24,64]{2,1,0:T(8,128)S(1)}, u32[]{:S(2)}, u32[]{:S(2)}) collective-permute-start(f32[1,24,64]{2,1,0:T(8,128)S(1)} %broadcast.116), channel_id=1, source_target_pairs={{0,4},{4,8},{8,12},{12,16},{16,20},{20,24},{24,28},{1,5},{5,9},{9,... | collective-permute-start | bytes 18440 | tf_op jit(solution)/shard_map/ppermute | solution.py:19
  70.8 22.4 %copy-start = (f32[32,32,128]{2,1,0:T(8,128)S(1)}, f32[32,32,128]{2,1,0:T(8,128)}, u32[]{:S(2)}) copy-start(f32[32,32,128]{2,1,0:T(8,128)} %param.3) | copy-start | bytes 1572868
  70.8 6.9 %collective-permute-start.4 = (f32[1,32,128]{2,1,0:T(8,128)S(1)}, f32[1,32,128]{2,1,0:T(8,128)S(1)}, u32[]{:S(2)}, u32[]{:S(2)}) collective-permute-start(f32[1,32,128]{2,1,0:T(8,128)S(1)} %get-tuple-element.17), channel_id=1, source_target_pairs={{4,0},{8,4},{12,8},{16,12},{20,16},{24,20},{28,24},{5,1},{9,5},{13... | collective-permute-start | bytes 49160 | tf_op jit(solution)/shard_map/ppermute | solution.py:21
  75.7 5.1 %collective-permute-start.5 = (f32[1,32,128]{2,1,0:T(8,128)S(1)}, f32[1,32,128]{2,1,0:T(8,128)S(1)}, u32[]{:S(2)}, u32[]{:S(2)}) collective-permute-start(f32[1,32,128]{2,1,0:T(8,128)S(1)} %get-tuple-element.16), channel_id=1, source_target_pairs={{0,4},{4,8},{8,12},{12,16},{16,20},{20,24},{24,28},{1,5},{5,9},{9,... | collective-permute-start | bytes 49160 | tf_op jit(solution)/shard_map/ppermute | solution.py:19
  80.8 7.2 %collective-permute-start.6 = (f32[34,1,128]{2,1,0:T(1,128)S(1)}, f32[34,1,128]{2,1,0:T(1,128)S(1)}, u32[]{:S(2)}, u32[]{:S(2)}) collective-permute-start(f32[34,1,128]{2,1,0:T(1,128)S(1)} %get-tuple-element.21), channel_id=1, source_target_pairs={{1,0},{2,1},{3,2},{5,4},{6,5},{7,6},{9,8},{10,9},{11,10},{13,12},{... | collective-permute-start | bytes 52232 | tf_op jit(solution)/shard_map/ppermute | solution.py:21
  86.0 6.5 %collective-permute-start.7 = (f32[34,1,128]{2,1,0:T(1,128)S(1)}, f32[34,1,128]{2,1,0:T(1,128)S(1)}, u32[]{:S(2)}, u32[]{:S(2)}) collective-permute-start(f32[34,1,128]{2,1,0:T(1,128)S(1)} %get-tuple-element.20), channel_id=1, source_target_pairs={{0,1},{1,2},{2,3},{4,5},{5,6},{6,7},{8,9},{9,10},{10,11},{12,13},{... | collective-permute-start | bytes 52232 | tf_op jit(solution)/shard_map/ppermute | solution.py:19
  140.7 7.0 %collective-permute-start.8 = (f32[16,4,64]{2,1,0:T(4,128)S(1)}, f32[16,4,64]{2,1,0:T(4,128)S(1)}, u32[]{:S(2)}, u32[]{:S(2)}) collective-permute-start(f32[16,4,64]{2,1,0:T(4,128)S(1)} %get-tuple-element.34), channel_id=1, source_target_pairs={{0,1},{1,2},{2,3},{4,5},{5,6},{6,7},{8,9},{9,10},{10,11},{12,13},{... | collective-permute-start | bytes 49160 | tf_op jit(solution)/shard_map/ppermute | solution.py:19
  142.6 6.4 %collective-permute-start.9 = (f32[16,4,64]{2,1,0:T(4,128)S(1)}, f32[16,4,64]{2,1,0:T(4,128)S(1)}, u32[]{:S(2)}, u32[]{:S(2)}) collective-permute-start(f32[16,4,64]{2,1,0:T(4,128)S(1)} %get-tuple-element.35), channel_id=1, source_target_pairs={{1,0},{2,1},{3,2},{5,4},{6,5},{7,6},{9,8},{10,9},{11,10},{13,12},{... | collective-permute-start | bytes 49160 | tf_op jit(solution)/shard_map/ppermute | solution.py:21
  149.3 4.3 %collective-permute-start.12 = (f32[1,24,64]{2,1,0:T(8,128)S(1)}, f32[1,24,64]{2,1,0:T(8,128)S(1)}, u32[]{:S(2)}, u32[]{:S(2)}) collective-permute-start(f32[1,24,64]{2,1,0:T(8,128)S(1)} %get-tuple-element.33), channel_id=1, source_target_pairs={{4,0},{8,4},{12,8},{16,12},{20,16},{24,20},{28,24},{5,1},{9,5},{13... | collective-permute-start | bytes 18440 | tf_op jit(solution)/shard_map/ppermute | solution.py:21
  151.3 5.0 %collective-permute-start.13 = (f32[1,24,64]{2,1,0:T(8,128)S(1)}, f32[1,24,64]{2,1,0:T(8,128)S(1)}, u32[]{:S(2)}, u32[]{:S(2)}) collective-permute-start(f32[1,24,64]{2,1,0:T(8,128)S(1)} %get-tuple-element.32), channel_id=1, source_target_pairs={{0,4},{4,8},{8,12},{12,16},{16,20},{20,24},{24,28},{1,5},{5,9},{9,... | collective-permute-start | bytes 18440 | tf_op jit(solution)/shard_map/ppermute | solution.py:19
  156.8 4.3 %collective-permute-start.14 = (f32[1,24,64]{2,1,0:T(8,128)S(1)}, f32[1,24,64]{2,1,0:T(8,128)S(1)}, u32[]{:S(2)}, u32[]{:S(2)}) collective-permute-start(f32[1,24,64]{2,1,0:T(8,128)S(1)} %get-tuple-element.31), channel_id=1, source_target_pairs={{4,0},{8,4},{12,8},{16,12},{20,16},{24,20},{28,24},{5,1},{9,5},{13... | collective-permute-start | bytes 18440 | tf_op jit(solution)/shard_map/ppermute | solution.py:21
  158.7 5.0 %collective-permute-start.15 = (f32[1,24,64]{2,1,0:T(8,128)S(1)}, f32[1,24,64]{2,1,0:T(8,128)S(1)}, u32[]{:S(2)}, u32[]{:S(2)}) collective-permute-start(f32[1,24,64]{2,1,0:T(8,128)S(1)} %get-tuple-element.30), channel_id=1, source_target_pairs={{0,4},{4,8},{8,12},{12,16},{16,20},{20,24},{24,28},{1,5},{5,9},{9,... | collective-permute-start | bytes 18440 | tf_op jit(solution)/shard_map/ppermute | solution.py:19
  164.2 4.7 %collective-permute-start.16 = (f32[1,24,64]{2,1,0:T(8,128)S(1)}, f32[1,24,64]{2,1,0:T(8,128)S(1)}, u32[]{:S(2)}, u32[]{:S(2)}) collective-permute-start(f32[1,24,64]{2,1,0:T(8,128)S(1)} %get-tuple-element.27), channel_id=1, source_target_pairs={{4,0},{8,4},{12,8},{16,12},{20,16},{24,20},{28,24},{5,1},{9,5},{13... | collective-permute-start | bytes 18440 | tf_op jit(solution)/shard_map/ppermute | solution.py:21
  166.1 5.0 %collective-permute-start.17 = (f32[1,24,64]{2,1,0:T(8,128)S(1)}, f32[1,24,64]{2,1,0:T(8,128)S(1)}, u32[]{:S(2)}, u32[]{:S(2)}) collective-permute-start(f32[1,24,64]{2,1,0:T(8,128)S(1)} %get-tuple-element.26), channel_id=1, source_target_pairs={{0,4},{4,8},{8,12},{12,16},{16,20},{20,24},{24,28},{1,5},{5,9},{9,... | collective-permute-start | bytes 18440 | tf_op jit(solution)/shard_map/ppermute | solution.py:19
  207.2 7.0 %collective-permute-start.18 = (f32[3,4,32,128]{3,2,1,0:T(8,128)S(1)}, f32[3,4,32,128]{3,2,1,0:T(8,128)S(1)}, u32[]{:S(2)}, u32[]{:S(2)}) collective-permute-start(f32[3,4,32,128]{3,2,1,0:T(8,128)S(1)} %get-tuple-element.10), channel_id=1, source_target_pairs={{0,4},{4,8},{8,12},{12,16},{16,20},{20,24},{24,28},{1,5},{5,9},{9,... | collective-permute-start | bytes 589832 | tf_op jit(solution)/shard_map/ppermute | solution.py:19
  209.2 6.8 %collective-permute-start.19 = (f32[3,4,32,128]{3,2,1,0:T(8,128)S(1)}, f32[3,4,32,128]{3,2,1,0:T(8,128)S(1)}, u32[]{:S(2)}, u32[]{:S(2)}) collective-permute-start(f32[3,4,32,128]{3,2,1,0:T(8,128)S(1)} %get-tuple-element.11), channel_id=1, source_target_pairs={{4,0},{8,4},{12,8},{16,12},{20,16},{24,20},{28,24},{5,1},{9,5},{13... | collective-permute-start | bytes 589832 | tf_op jit(solution)/shard_map/ppermute | solution.py:21
  216.3 11.3 %collective-permute-start.20 = (f32[3,40,4,128]{3,2,1,0:T(4,128)S(1)}, f32[3,40,4,128]{3,2,1,0:T(4,128)S(1)}, u32[]{:S(2)}, u32[]{:S(2)}) collective-permute-start(f32[3,40,4,128]{3,2,1,0:T(4,128)S(1)} %get-tuple-element.6), channel_id=1, source_target_pairs={{0,1},{1,2},{2,3},{4,5},{5,6},{6,7},{8,9},{9,10},{10,11},{12,13},{... | collective-permute-start | bytes 737288 | tf_op jit(solution)/shard_map/ppermute | solution.py:19
  218.2 9.3 %collective-permute-start.21 = (f32[3,40,4,128]{3,2,1,0:T(4,128)S(1)}, f32[3,40,4,128]{3,2,1,0:T(4,128)S(1)}, u32[]{:S(2)}, u32[]{:S(2)}) collective-permute-start(f32[3,40,4,128]{3,2,1,0:T(4,128)S(1)} %get-tuple-element.7), channel_id=1, source_target_pairs={{1,0},{2,1},{3,2},{5,4},{6,5},{7,6},{9,8},{10,9},{11,10},{13,12},{... | collective-permute-start | bytes 737288 | tf_op jit(solution)/shard_map/ppermute | solution.py:21
  232.0 6.7 %collective-permute-start.22 = (f32[1,32,128]{2,1,0:T(8,128)S(1)}, f32[1,32,128]{2,1,0:T(8,128)S(1)}, u32[]{:S(2)}, u32[]{:S(2)}) collective-permute-start(f32[1,32,128]{2,1,0:T(8,128)S(1)} %get-tuple-element.15), channel_id=1, source_target_pairs={{4,0},{8,4},{12,8},{16,12},{20,16},{24,20},{28,24},{5,1},{9,5},{13... | collective-permute-start | bytes 49160 | tf_op jit(solution)/shard_map/ppermute | solution.py:21
  236.7 5.1 %collective-permute-start.23 = (f32[1,32,128]{2,1,0:T(8,128)S(1)}, f32[1,32,128]{2,1,0:T(8,128)S(1)}, u32[]{:S(2)}, u32[]{:S(2)}) collective-permute-start(f32[1,32,128]{2,1,0:T(8,128)S(1)} %get-tuple-element.14), channel_id=1, source_target_pairs={{0,4},{4,8},{8,12},{12,16},{16,20},{20,24},{24,28},{1,5},{5,9},{9,... | collective-permute-start | bytes 49160 | tf_op jit(solution)/shard_map/ppermute | solution.py:19
  238.7 16.6 %copy-start.1 = (f32[32,32,128]{2,1,0:T(8,128)}, f32[32,32,128]{2,1,0:T(8,128)S(1)}, u32[]{:S(2)}) copy-start(f32[32,32,128]{2,1,0:T(8,128)S(1)} %slice.558) | copy-start | bytes 1572868
  241.8 7.1 %collective-permute-start.24 = (f32[34,1,128]{2,1,0:T(1,128)S(1)}, f32[34,1,128]{2,1,0:T(1,128)S(1)}, u32[]{:S(2)}, u32[]{:S(2)}) collective-permute-start(f32[34,1,128]{2,1,0:T(1,128)S(1)} %get-tuple-element.19), channel_id=1, source_target_pairs={{1,0},{2,1},{3,2},{5,4},{6,5},{7,6},{9,8},{10,9},{11,10},{13,12},{... | collective-permute-start | bytes 52232 | tf_op jit(solution)/shard_map/ppermute | solution.py:21
  246.9 6.5 %collective-permute-start.25 = (f32[34,1,128]{2,1,0:T(1,128)S(1)}, f32[34,1,128]{2,1,0:T(1,128)S(1)}, u32[]{:S(2)}, u32[]{:S(2)}) collective-permute-start(f32[34,1,128]{2,1,0:T(1,128)S(1)} %get-tuple-element.18), channel_id=1, source_target_pairs={{0,1},{1,2},{2,3},{4,5},{5,6},{6,7},{8,9},{9,10},{10,11},{12,13},{... | collective-permute-start | bytes 52232 | tf_op jit(solution)/shard_map/ppermute | solution.py:19
where the time goes:
time: 257 us; the launch traced here: 255 us
  starting transfers between devices  77.7 us (30%)
  local copies, waits for them, and re-layouts  71 us (28%)
  blocking collectives  40.2 us (16%)
  waiting for transfers between devices  34.6 us (13%)
  other arithmetic  29.7 us (12%)
    ppermute x13, starting transfers between devices, with_halo(): lax.ppermute(head, axis, [((i + 1) % count, i) for i in range(ends)])  50.5 us
    psum x1, blocking collectives, per_device(): density_mean = lax.psum(jnp.sum(source), ('group', 'member')) / total_cells  40.2 us
    reshape x1, local copies, waits for them, and re-layouts, per_device(): fine_residual.reshape(half_x, 2, half_y, 2, half_z, 2).sum(axis=(1, 3, 5))  34.9 us
    ppermute x13, waiting for transfers between devices, with_halo(): lax.ppermute(tail, axis, [(i, (i + 1) % count) for i in range(ends)])  29.7 us
    ppermute x13, starting transfers between devices, with_halo(): lax.ppermute(tail, axis, [(i, (i + 1) % count) for i in range(ends)])  27.1 us
    reshape x1, local copies, waits for them, and re-layouts, expand(): return wide.reshape(size_a * factor, size_b * factor, size_c * factor)  24 us
    reduce_sum x1, other arithmetic, per_device(): fine_residual.reshape(half_x, 2, half_y, 2, half_z, 2).sum(axis=(1, 3, 5))  12.2 us
    broadcast_in_dim x3, local copies, waits for them, and re-layouts, expand(): jnp.broadcast_to(values_in[:, None, :, None, :, None], (size_a, factor, s...  11.5 us
  transfers between devices with their start and end apart: 26, of which 13 were waited for; matrix products, arithmetic and copies ran while one was open for 21% of the time, Pallas kernels for 0%

commit v1 on v0

v1 whole, which is shorter than its diff:
```python
import functools

import jax
import jax.numpy as jnp
from jax import lax
from jax.experimental import pallas as pl
from jax.experimental.pallas import tpu as pltpu
from jax.sharding import PartitionSpec as P

PRE = 2
POST = 2
COARSE = 2
SWEEP_DEPTH = 2 * max(PRE, POST)
DEPTH = SWEEP_DEPTH + 1
COARSE_DEPTH = 2 * COARSE - 1 + (DEPTH + 1) // 2
ROW0 = 8 + SWEEP_DEPTH
COARSE_ROW0 = 16
SIDES = ((0, -1), (0, 1), (-1, -1), (-1, 1), (1, -1), (1, 1), (-1, 0), (1, 0))
MESH = pl.DeviceIdType.MESH


def slabs(side, count, offset, depth):
    if side == 0:
        return pl.ds(offset, count), pl.ds(offset, count)
    if side < 0:
        return pl.ds(offset, depth), pl.ds(offset + count, depth)
    return pl.ds(offset + count - depth, depth), pl.ds(offset - depth, depth)


def halo_slabs(side, count, offset, depth):
    return pl.ds(offset, count) if side == 0 else slabs(-side, count, offset, depth)[1]


def kernel(
    dims, sizes,
    refined_ref, source_ref, potential_ref,
    smoothed_ref, residual_ref,
    fine, rhs, post, coarse, corr, flags, weights, coarse_weights, pair_rows, wide_rows, res_rows,
    member_sums, group_sums,
    local_sem, send_sem, recv_sem, msum_send, msum_recv, gsum_send, gsum_recv,
):
    groups, members = dims
    cx, cy, cz = sizes
    hx, hy = cx // 2, cy // 2
    group_at = lax.axis_index("group")
    member_at = lax.axis_index("member")
    work = cy + 2 * SWEEP_DEPTH
    coarse_work = hy + 16
    own_rows = pl.ds(ROW0, cy)
    own_planes = pl.ds(DEPTH, cx)

    load_rhs = pltpu.make_async_copy(source_ref, rhs.at[own_planes, own_rows], local_sem.at[0])
    load_fine = pltpu.make_async_copy(potential_ref, fine.at[own_planes, own_rows], local_sem.at[1])
    load_rhs.start()
    load_fine.start()

    def there(dx, dy):
        ok = None
        for side, at, count in ((dx, group_at, groups), (dy, member_at, members)):
            if side == 0:
                continue
            here = at > 0 if side < 0 else at < count - 1
            ok = here if ok is None else ok & here
        return ok

    def device(dx, dy):
        return (group_at + dx, member_at + dy)

    barrier = pltpu.get_barrier_semaphore()
    for o in range(1, members):
        pl.semaphore_signal(barrier, inc=1, device_id=(group_at, lax.rem(member_at + o, members)), device_id_type=MESH)
    for o in range(1, groups):
        pl.semaphore_signal(barrier, inc=1, device_id=(lax.rem(group_at + o, groups), member_at), device_id_type=MESH)
    expected = jnp.int32(groups - 1 + members - 1)
    for dx, dy in SIDES:
        if dx and dy:
            @pl.when(there(dx, dy))
            def _():
                pl.semaphore_signal(barrier, inc=1, device_id=device(dx, dy), device_id_type=MESH)
            expected = expected + there(dx, dy).astype(jnp.int32)

    lane8 = lax.broadcasted_iota(jnp.int32, (8, cz), 1)
    boxes = refined_ref.shape[2]
    box = cz // boxes
    marks = jnp.zeros((8, cz), jnp.int32)
    for b in range(boxes):
        marks = jnp.where(lane8 // box == b, jnp.full((8, cz), refined_ref[0, 0, b], jnp.int32), marks)
    flags[1, 1] = (marks == 1).astype(jnp.float32)

    for dx, dy in SIDES:
        @pl.when(jnp.logical_not(there(dx, dy)))
        def _():
            flags[1 + dx, 1 + dy] = jnp.zeros((8, cz), jnp.float32)
            px = halo_slabs(dx, cx, DEPTH, DEPTH)
            py = halo_slabs(dy, cy, ROW0, DEPTH)
            blank = jnp.zeros((py.size, cz), jnp.float32)

            def clear(i, carry):
                fine[px.start + i, py, :] = blank
                post[px.start + i, py, :] = blank
                return carry

            lax.fori_loop(0, px.size, clear, 0)

    crow = lax.broadcasted_iota(jnp.int32, (coarse_work, cz), 0) - (COARSE_ROW0 - 8)
    clane = lax.broadcasted_iota(jnp.int32, (coarse_work, cz), 1)
    clow = jnp.where(member_at > 0, -COARSE_DEPTH, 0)
    chigh = jnp.where(member_at < members - 1, hy + COARSE_DEPTH, hy)
    cinside = (crow >= clow) & (crow < chigh)
    cbase = (crow + clane // 2) & 1
    for region in range(3):
        if region == 1:
            keep = cinside
        else:
            alive = there(region - 1, 0).astype(jnp.int32)
            keep = cinside & (jnp.full(crow.shape, alive, jnp.int32) == 1)
        for q in range(2):
            coarse_weights[region, q] = (keep & (cbase == q)).astype(jnp.float32)

    load_rhs.wait()

    def add_plane(i, acc):
        for t in range(cy // 8):
            acc = acc + rhs[DEPTH + i, pl.ds(ROW0 + 8 * t, 8), :]
        return acc

    member_sums[0] = lax.fori_loop(0, cx, add_plane, jnp.zeros((8, cz), jnp.float32))
    load_fine.wait()
    pl.semaphore_wait(barrier, expected)

    def sum_copies(slots, send, recv, count, target):
        return [
            pltpu.make_async_remote_copy(
                src_ref=slots.at[0], dst_ref=slots.at[o], send_sem=send.at[o], recv_sem=recv.at[o],
                device_id=target(o), device_id_type=MESH,
            )
            for o in range(1, count)
        ]

    msum = sum_copies(member_sums, msum_send, msum_recv, members, lambda o: (group_at, lax.rem(member_at + o, members)))
    gsum = sum_copies(group_sums, gsum_send, gsum_recv, groups, lambda o: (lax.rem(group_at + o, groups), member_at))
    for c in msum:
        c.start()

    def halo_copy(kind, n, src, dst, counts, offsets, depth):
        dx, dy = SIDES[n]
        sx, tx = slabs(dx, counts[0], offsets[0], depth)
        sy, ty = slabs(dy, counts[1], offsets[1], depth)
        return pltpu.make_async_remote_copy(
            src_ref=src.at[sx, sy], dst_ref=dst.at[tx, ty],
            send_sem=send_sem.at[kind, n], recv_sem=recv_sem.at[kind, n],
            device_id=device(dx, dy), device_id_type=MESH,
        )

    def first_round(n):
        dx, dy = SIDES[n]
        return [
            pltpu.make_async_remote_copy(
                src_ref=flags.at[1, 1], dst_ref=flags.at[1 - dx, 1 - dy],
                send_sem=send_sem.at[0, n], recv_sem=recv_sem.at[0, n],
                device_id=device(dx, dy), device_id_type=MESH,
            ),
            halo_copy(1, n, fine, fine, (cx, cy), (DEPTH, ROW0), DEPTH),
            halo_copy(2, n, rhs, rhs, (cx, cy), (DEPTH, ROW0), SWEEP_DEPTH),
        ]

    def second_coarse(n):
        return [halo_copy(3, n, coarse, coarse, (hx, hy), (COARSE_DEPTH, COARSE_ROW0), COARSE_DEPTH)]

    def second_fine(n):
        return [halo_copy(4, n, fine, post, (cx, cy), (DEPTH, ROW0), DEPTH)]

    def start(round_of):
        for n, (dx, dy) in enumerate(SIDES):
            @pl.when(there(dx, dy))
            def _():
                for c in round_of(n):
                    c.start()

    def arrive(round_of):
        for n, (dx, dy) in enumerate(SIDES):
            @pl.when(there(-dx, -dy))
            def _():
                for c in round_of(n):
                    c.wait_recv()

    def sent(round_of):
        for n, (dx, dy) in enumerate(SIDES):
            @pl.when(there(dx, dy))
            def _():
                for c in round_of(n):
                    c.wait_send()

    start(first_round)

    for c in msum:
        c.wait_recv()
    part = member_sums[0]
    for o in range(1, members):
        part = part + member_sums[o]
    group_sums[0] = part
    for c in gsum:
        c.start()
    for c in gsum:
        c.wait_recv()
    total = group_sums[0]
    for o in range(1, groups):
        total = total + group_sums[o]
    mean = jnp.sum(total) / (cx * cy * cz * groups * members)

    arrive(first_round)
    sent(first_round)

    frow = lax.broadcasted_iota(jnp.int32, (work, cz), 0) - SWEEP_DEPTH
    flane = lax.broadcasted_iota(jnp.int32, (work, cz), 1)
    fbase = (frow + flane) & 1
    for region in range(3):
        here = jnp.where(
            frow < 0, flags[region, 0, 0:1, :], jnp.where(frow < cy, flags[region, 1, 0:1, :], flags[region, 2, 0:1, :])
        )
        for q in range(2):
            weights[region, q] = jnp.where(fbase == q, here, 0.0)

    def lanes(value, step):
        lane = lax.broadcasted_iota(jnp.int32, value.shape, 1)
        low = jnp.where(lane < step, 0.0, pltpu.roll(value, step, 1))
        high = jnp.where(lane >= cz - step, 0.0, pltpu.roll(value, cz - step, 1))
        return low + high

    def around(field, i, row, rows, step):
        centre = field[i, pl.ds(row, rows), :]
        total = field[i - 1, pl.ds(row, rows), :] + field[i + 1, pl.ds(row, rows), :]
        total = total + (field[i, pl.ds(row - 1, rows), :] + field[i, pl.ds(row + 1, rows), :])
        return centre, total + lanes(centre, step)

    def smooth(field, count):
        for t in range(2 * count):
            reach = 2 * count - t

            def one(i, carry):
                region = (i >= DEPTH).astype(jnp.int32) + (i >= DEPTH + cx).astype(jnp.int32)
                parity = lax.rem(i + DEPTH + t, 2)
                centre, nbr = around(field, i, 8, work, 1)
                update = (rhs[i, pl.ds(8, work), :] - mean + nbr) * (1.0 / 6.0)
                field[i, pl.ds(8, work), :] = jnp.where(weights[region, parity] > 0.5, update, centre)
                return carry

            lax.fori_loop(DEPTH - reach, DEPTH + cx + reach, one, 0)

    smooth(fine, PRE)

    lane = lax.broadcasted_iota(jnp.int32, (cy, cz), 1)
    even = lane % 2 == 0

    def defect(field, i):
        centre, nbr = around(field, i, ROW0, cy, 1)
        return centre, rhs[i, own_rows, :] - mean - (6.0 * centre - nbr)

    def restrict(a, carry):
        i = DEPTH + 2 * a
        first, res_a = defect(fine, i)
        second, res_b = defect(fine, i + 1)
        post[i, own_rows, :] = first
        post[i + 1, own_rows, :] = second
        both = res_a + res_b
        both = both + jnp.where(even, pltpu.roll(both, cz - 1, 1), pltpu.roll(both, 1, 1))
        pair_rows[a] = both
        coarse[COARSE_DEPTH + a, pl.ds(COARSE_ROW0, hy), :] = 0.5 * (
            pair_rows[a, pl.ds(0, hy, stride=2), :] + pair_rows[a, pl.ds(1, hy, stride=2), :]
        )
        return carry

    lax.fori_loop(0, hx, restrict, 0)

    start(second_coarse)
    start(second_fine)
    arrive(second_coarse)
    sent(second_coarse)

    planes = hx + 2 * COARSE_DEPTH

    def coarse_region(i):
        return (i >= COARSE_DEPTH).astype(jnp.int32) + (i >= COARSE_DEPTH + hx).astype(jnp.int32)

    def coarse_first(i, carry):
        w = coarse_weights[coarse_region(i), lax.rem(i + COARSE_DEPTH, 2)]
        corr[i, pl.ds(8, coarse_work), :] = jnp.where(w > 0.5, coarse[i, pl.ds(8, coarse_work), :] * (1.0 / 6.0), 0.0)
        return carry

    lax.fori_loop(0, planes, coarse_first, 0)
    for t in range(1, 2 * COARSE):
        def coarse_one(i, carry):
            w = coarse_weights[coarse_region(i), lax.rem(i + COARSE_DEPTH + t, 2)]
            centre, nbr = around(corr, i, 8, coarse_work, 2)
            update = (coarse[i, pl.ds(8, coarse_work), :] + nbr) * (1.0 / 6.0)
            corr[i, pl.ds(8, coarse_work), :] = jnp.where(w > 0.5, update, centre)
            return carry

        lax.fori_loop(t, planes - t, coarse_one, 0)

    arrive(second_fine)
    sent(second_fine)

    half_rows = hy + 8
    first_plane = 2 * COARSE - 1

    def add_correction(c, carry):
        plane = corr[c, pl.ds(COARSE_ROW0 - 4, half_rows), :]
        wide_rows[c, pl.ds(0, half_rows, stride=2), :] = plane
        wide_rows[c, pl.ds(1, half_rows, stride=2), :] = plane
        wide = wide_rows[c]
        for b in range(2):
            i = 2 * (c - COARSE_DEPTH) + DEPTH + b
            post[i, pl.ds(ROW0 - 8, cy + 16), :] = post[i, pl.ds(ROW0 - 8, cy + 16), :] + wide
        return carry

    def add_end(c, b):
        plane = corr[c, pl.ds(COARSE_ROW0 - 4, half_rows), :]
        wide_rows[c, pl.ds(0, half_rows, stride=2), :] = plane
        wide_rows[c, pl.ds(1, half_rows, stride=2), :] = plane
        i = 2 * (c - COARSE_DEPTH) + DEPTH + b
        post[i, pl.ds(ROW0 - 8, cy + 16), :] = post[i, pl.ds(ROW0 - 8, cy + 16), :] + wide_rows[c]

    add_end(first_plane, 1)
    lax.fori_loop(first_plane + 1, planes - first_plane - 1, add_correction, 0)
    add_end(planes - first_plane - 1, 0)

    smooth(post, POST)
    store_smoothed = pltpu.make_async_copy(post.at[own_planes, own_rows], smoothed_ref, local_sem.at[0])
    store_smoothed.start()

    def last(i, carry):
        res_rows[i] = defect(post, DEPTH + i)[1]
        return carry

    lax.fori_loop(0, cx, last, 0)
    store_residual = pltpu.make_async_copy(res_rows, residual_ref, local_sem.at[1])
    store_residual.start()
    for c in msum + gsum:
        c.wait_send()
    store_smoothed.wait()
    store_residual.wait()


def per_device(dims, source, potential, refined):
    cx, cy, cz = source.shape
    groups, members = dims
    hx, hy = cx // 2, cy // 2
    wide = (cx + 2 * DEPTH, ROW0 + cy + ROW0, cz)
    narrow = (hx + 2 * COARSE_DEPTH, hy + 2 * COARSE_ROW0, cz)
    f32 = jnp.float32
    dma = pltpu.SemaphoreType.DMA
    any_spec = pl.BlockSpec(memory_space=pl.ANY)
    return tuple(pl.pallas_call(
        functools.partial(kernel, dims, (cx, cy, cz)),
        out_shape=[jax.ShapeDtypeStruct(source.shape, f32)] * 2,
        in_specs=[pl.BlockSpec(memory_space=pltpu.SMEM), any_spec, any_spec],
        out_specs=[any_spec, any_spec],
        scratch_shapes=[
            pltpu.VMEM(wide, f32),
            pltpu.VMEM(wide, f32),
            pltpu.VMEM(wide, f32),
            pltpu.VMEM(narrow, f32),
            pltpu.VMEM(narrow, f32),
            pltpu.VMEM((3, 3, 8, cz), f32),
            pltpu.VMEM((3, 2, cy + 2 * SWEEP_DEPTH, cz), f32),
            pltpu.VMEM((3, 2, hy + 16, cz), f32),
            pltpu.VMEM((hx, cy, cz), f32),
            pltpu.VMEM((narrow[0], cy + 16, cz), f32),
            pltpu.VMEM((cx, cy, cz), f32),
            pltpu.VMEM((members, 8, cz), f32),
            pltpu.VMEM((groups, 8, cz), f32),
            dma((2,)),
            dma((5, len(SIDES))),
            dma((5, len(SIDES))),
            dma((members,)),
            dma((members,)),
            dma((groups,)),
            dma((groups,)),
        ],
        compiler_params=pltpu.CompilerParams(collective_id=0, has_side_effects=True),
    )(refined, source, potential))


def solution(mesh):
    spec = P("group", "member", None)
    return jax.shard_map(
        functools.partial(per_device, (mesh.shape["group"], mesh.shape["member"])),
        mesh=mesh,
        in_specs=(spec, spec, spec),
        out_specs=(spec, spec),
        check_vma=False,
    )
```

time: 257 us -> 63.8 us (0.25)
  the two profiles are of different devices: /device:TPU:28 before, /device:TPU:0 now
where the time goes in v1:
time: 63.8 us; the launch traced here: 63.7 us
  Pallas kernels  60.3 us (95%)
  local copies, waits for them, and re-layouts  2.72 us (4%)
  between operations  0.65 us (1%)
    pallas_call x1, Pallas kernels, per_device(): pl.pallas_call(functools.partial(kernel, dims, (cx, cy, cz)), out_shape=[...  60.3 us
    unnamed x4, local copies, waits for them, and re-layouts  2.72 us

profile of v1, /device:TPU:0, one launch (start us, length us, event | category | flops | bytes accessed | tf_op | source)
XLA Modules:
  0.0 63.7 jit_solution(12127969201671251857)
XLA Ops:
  0.6 60.3 %shard_map.50 = (f32[32,32,128]{2,1,0:T(8,128)}, f32[32,32,128]{2,1,0:T(8,128)}) custom-call(s32[1,1,4]{2,1,0:T(1,128)} %refined_ref.1, f32[32,32,128]{2,1,0:T(8,128)} %source_ref.1, f32[32,32,128]{2,1,0:T(8,128)} %potential_ref.1), custom_call_target="tpu_custom_call" | custom-call | tf_op jit(solution)/shard_map/pallas_call | solution.py:354
  60.9 0.0 copy-start
  60.9 1.9 %copy.7 = f32[32,32,128]{2,1,0:T(8,128)} copy(f32[32,32,128]{2,1,0:T(8,128)} %get-tuple-element.4) | data formatting | bytes 1048576
  62.9 0.0 copy-done
  62.9 0.8 %copy.8 = f32[32,32,128]{2,1,0:T(8,128)} copy(f32[32,32,128]{2,1,0:T(8,128)S(1)} %copy-done) | data formatting | bytes 1048576
Async XLA Ops:
  60.9 1.9 %copy-start = (f32[32,32,128]{2,1,0:T(8,128)S(1)}, f32[32,32,128]{2,1,0:T(8,128)}, u32[]{:S(2)}) copy-start(f32[32,32,128]{2,1,0:T(8,128)} %get-tuple-element.5) | copy-start | bytes 1572868

commit v2 on v1

--- a/solution.py
+++ b/solution.py
@@ -15,27 +15,45 @@
 COARSE_DEPTH = 2 * COARSE - 1 + (DEPTH + 1) // 2
 ROW0 = 8 + SWEEP_DEPTH
 COARSE_ROW0 = 16
+GROUP = 8
+STEPS = COARSE_DEPTH
 SIDES = ((0, -1), (0, 1), (-1, -1), (-1, 1), (1, -1), (1, 1), (-1, 0), (1, 0))
 MESH = pl.DeviceIdType.MESH
 
 
-def slabs(side, count, offset, depth):
+def slabs(side, count, offset, skip, depth):
     if side == 0:
         return pl.ds(offset, count), pl.ds(offset, count)
     if side < 0:
-        return pl.ds(offset, depth), pl.ds(offset + count, depth)
-    return pl.ds(offset + count - depth, depth), pl.ds(offset - depth, depth)
+        return pl.ds(offset + skip, depth - skip), pl.ds(offset + count + skip, depth - skip)
+    return pl.ds(offset + count - depth, depth - skip), pl.ds(offset - depth, depth - skip)
+
+
+def corner_steps(depth):
+    steps = []
+    at = 0
+    while at < depth - 1:
+        width = 1 if (depth - 1 - at) % 2 else 2
+        steps.append((at, at + width, depth - 1 - at))
+        at += width
+    return steps
 
 
 def halo_slabs(side, count, offset, depth):
-    return pl.ds(offset, count) if side == 0 else slabs(-side, count, offset, depth)[1]
+    return pl.ds(offset, count) if side == 0 else slabs(-side, count, offset, 0, depth)[1]
+
+
+def region_of(at, offset, count):
+    if isinstance(at, int):
+        return int(at >= offset) + int(at >= offset + count)
+    return (at >= offset).astype(jnp.int32) + (at >= offset + count).astype(jnp.int32)
 
 
 def kernel(
     dims, sizes,
     refined_ref, source_ref, potential_ref,
     smoothed_ref, residual_ref,
-    fine, rhs, post, coarse, corr, flags, weights, coarse_weights, pair_rows, wide_rows, res_rows,
+    fine, rhs, post, coarse, corr, packed, flags, weights, coarse_weights, pair_rows, wide_rows, res_rows,
     member_sums, group_sums,
     local_sem, send_sem, recv_sem, msum_send, msum_recv, gsum_send, gsum_recv,
 ):
@@ -142,15 +160,19 @@
     for c in msum:
         c.start()
 
-    def halo_copy(kind, n, src, dst, counts, offsets, depth):
+    def halo_copies(kind, n, src, dst, counts, offsets, depth, skip=0):
         dx, dy = SIDES[n]
-        sx, tx = slabs(dx, counts[0], offsets[0], depth)
-        sy, ty = slabs(dy, counts[1], offsets[1], depth)
-        return pltpu.make_async_remote_copy(
-            src_ref=src.at[sx, sy], dst_ref=dst.at[tx, ty],
-            send_sem=send_sem.at[kind, n], recv_sem=recv_sem.at[kind, n],
-            device_id=device(dx, dy), device_id_type=MESH,
-        )
+        steps = corner_steps(depth) if dx and dy else [(skip, depth, depth)]
+        copies = []
+        for m, (begin, end, reach) in enumerate(steps):
+            sx, tx = slabs(dx, counts[0], offsets[0], begin, end)
+            sy, ty = slabs(dy, counts[1], offsets[1], 0 if dx else skip, reach)
+            copies.append(pltpu.make_async_remote_copy(
+                src_ref=src.at[sx, sy], dst_ref=dst.at[tx, ty],
+                send_sem=send_sem.at[kind + m, n], recv_sem=recv_sem.at[kind + m, n],
+                device_id=device(dx, dy), device_id_type=MESH,
+            ))
+        return copies
 
     def first_round(n):
         dx, dy = SIDES[n]
@@ -160,15 +182,25 @@
                 send_sem=send_sem.at[0, n], recv_sem=recv_sem.at[0, n],
                 device_id=device(dx, dy), device_id_type=MESH,
             ),
-            halo_copy(1, n, fine, fine, (cx, cy), (DEPTH, ROW0), DEPTH),
-            halo_copy(2, n, rhs, rhs, (cx, cy), (DEPTH, ROW0), SWEEP_DEPTH),
-        ]
+        ] + (
+            halo_copies(1, n, fine, fine, (cx, cy), (DEPTH, ROW0), DEPTH)
+            + halo_copies(1 + STEPS, n, rhs, rhs, (cx, cy), (DEPTH, ROW0), SWEEP_DEPTH)
+        )
+
+    half_planes = hx // 2
 
     def second_coarse(n):
-        return [halo_copy(3, n, coarse, coarse, (hx, hy), (COARSE_DEPTH, COARSE_ROW0), COARSE_DEPTH)]
+        dx, dy = SIDES[n]
+        if dx:
+            return halo_copies(1 + 2 * STEPS, n, coarse, coarse, (hx, hy), (COARSE_DEPTH, COARSE_ROW0), COARSE_DEPTH)
+        return [pltpu.make_async_remote_copy(
+            src_ref=packed.at[1 + dy, pl.ds(0, half_planes)], dst_ref=packed.at[1 + dy, pl.ds(half_planes, half_planes)],
+            send_sem=send_sem.at[1 + 2 * STEPS, n], recv_sem=recv_sem.at[1 + 2 * STEPS, n],
+            device_id=device(dx, dy), device_id_type=MESH,
+        )]
 
     def second_fine(n):
-        return [halo_copy(4, n, fine, post, (cx, cy), (DEPTH, ROW0), DEPTH)]
+        return halo_copies(1 + 3 * STEPS, n, fine, post, (cx, cy), (DEPTH, ROW0), DEPTH, 1)
 
     def start(round_of):
         for n, (dx, dy) in enumerate(SIDES):
@@ -227,76 +259,117 @@
         high = jnp.where(lane >= cz - step, 0.0, pltpu.roll(value, cz - step, 1))
         return low + high
 
-    def around(field, i, row, rows, step):
-        centre = field[i, pl.ds(row, rows), :]
-        total = field[i - 1, pl.ds(row, rows), :] + field[i + 1, pl.ds(row, rows), :]
-        total = total + (field[i, pl.ds(row - 1, rows), :] + field[i, pl.ds(row + 1, rows), :])
-        return centre, total + lanes(centre, step)
+    def stencil(field, i, count, row, rows, step):
+        planes = [field[i + k, pl.ds(row, rows), :] for k in range(-1, count + 1)]
+        sums = []
+        for k in range(count):
+            total = planes[k] + planes[k + 2] + lanes(planes[k + 1], step)
+            total = total + (field[i + k, pl.ds(row - 1, rows), :] + field[i + k, pl.ds(row + 1, rows), :])
+            sums.append(total)
+        return planes[1:-1], sums
+
+    def in_groups(low, high, size, one):
+        whole = (high - low) // size
+
+        def body(g, carry):
+            one(low + g * size, size, low)
+            return carry
+
+        lax.fori_loop(0, whole, body, 0)
+        if (high - low) % size:
+            one(low + whole * size, (high - low) % size, low)
 
     def smooth(field, count):
         for t in range(2 * count):
             reach = 2 * count - t
 
-            def one(i, carry):
-                region = (i >= DEPTH).astype(jnp.int32) + (i >= DEPTH + cx).astype(jnp.int32)
-                parity = lax.rem(i + DEPTH + t, 2)
-                centre, nbr = around(field, i, 8, work, 1)
-                update = (rhs[i, pl.ds(8, work), :] - mean + nbr) * (1.0 / 6.0)
-                field[i, pl.ds(8, work), :] = jnp.where(weights[region, parity] > 0.5, update, centre)
-                return carry
-
-            lax.fori_loop(DEPTH - reach, DEPTH + cx + reach, one, 0)
+            def one(i, size, low):
+                centres, sums = stencil(field, i, size, 8, work, 1)
+                fresh = []
+                for k in range(size):
+                    at = i + k
+                    mask = weights[region_of(at, DEPTH, cx), (low + k + DEPTH + t) % 2] > 0.5
+                    update = (rhs[at, pl.ds(8, work), :] - mean + sums[k]) * (1.0 / 6.0)
+                    fresh.append(jnp.where(mask, update, centres[k]))
+                for k in range(size):
+                    field[i + k, pl.ds(8, work), :] = fresh[k]
+
+            in_groups(DEPTH - reach, DEPTH + cx + reach, GROUP, one)
 
     smooth(fine, PRE)
 
     lane = lax.broadcasted_iota(jnp.int32, (cy, cz), 1)
     even = lane % 2 == 0
 
-    def defect(field, i):
-        centre, nbr = around(field, i, ROW0, cy, 1)
-        return centre, rhs[i, own_rows, :] - mean - (6.0 * centre - nbr)
-
-    def restrict(a, carry):
+    def defects(field, i, count):
+        centres, sums = stencil(field, i, count, ROW0, cy, 1)
+        return centres, [rhs[i + k, own_rows, :] - mean - (6.0 * centres[k] - sums[k]) for k in range(count)]
+
+    def restrict(a, size, low):
         i = DEPTH + 2 * a
-        first, res_a = defect(fine, i)
-        second, res_b = defect(fine, i + 1)
-        post[i, own_rows, :] = first
-        post[i + 1, own_rows, :] = second
-        both = res_a + res_b
-        both = both + jnp.where(even, pltpu.roll(both, cz - 1, 1), pltpu.roll(both, 1, 1))
-        pair_rows[a] = both
-        coarse[COARSE_DEPTH + a, pl.ds(COARSE_ROW0, hy), :] = 0.5 * (
-            pair_rows[a, pl.ds(0, hy, stride=2), :] + pair_rows[a, pl.ds(1, hy, stride=2), :]
-        )
-        return carry
-
-    lax.fori_loop(0, hx, restrict, 0)
+        centres, res = defects(fine, i, 2 * size)
+        for k in range(size):
+            both = res[2 * k] + res[2 * k + 1]
+            both = both + jnp.where(even, pltpu.roll(both, cz - 1, 1), pltpu.roll(both, 1, 1))
+            pair_rows[a + k] = both
+        for k in range(2 * size):
+            post[i + k, own_rows, :] = centres[k]
+            post[i + k, pl.ds(ROW0 - 1, 1), :] = fine[i + k, pl.ds(ROW0 - 1, 1), :]
+            post[i + k, pl.ds(ROW0 + cy, 1), :] = fine[i + k, pl.ds(ROW0 + cy, 1), :]
+        for k in range(size):
+            coarse[COARSE_DEPTH + a + k, pl.ds(COARSE_ROW0, hy), :] = 0.5 * (
+                pair_rows[a + k, pl.ds(0, hy, stride=2), :] + pair_rows[a + k, pl.ds(1, hy, stride=2), :]
+            )
+
+    in_groups(0, hx, 2, restrict)
+
+    leven = lax.broadcasted_iota(jnp.int32, (COARSE_DEPTH, cz), 1) % 2 == 0
+    for dy in (-1, 1):
+        sy = slabs(dy, hy, COARSE_ROW0, 0, COARSE_DEPTH)[0]
+        for k in range(half_planes):
+            packed[1 + dy, k] = jnp.where(
+                leven, coarse[COARSE_DEPTH + k, sy, :], coarse[COARSE_DEPTH + half_planes + k, sy, :]
+            )
 
     start(second_coarse)
+    for i in (DEPTH - 1, DEPTH + cx):
+        post[i, own_rows, :] = fine[i, own_rows, :]
     start(second_fine)
     arrive(second_coarse)
     sent(second_coarse)
+    for dy in (-1, 1):
+        ty = slabs(dy, hy, COARSE_ROW0, 0, COARSE_DEPTH)[1]
+
+        @pl.when(there(0, -dy))
+        def _():
+            for k in range(half_planes):
+                both = packed[1 + dy, half_planes + k]
+                coarse[COARSE_DEPTH + k, ty, :] = jnp.where(leven, both, pltpu.roll(both, 1, 1))
+                coarse[COARSE_DEPTH + half_planes + k, ty, :] = jnp.where(leven, pltpu.roll(both, cz - 1, 1), both)
 
     planes = hx + 2 * COARSE_DEPTH
 
-    def coarse_region(i):
-        return (i >= COARSE_DEPTH).astype(jnp.int32) + (i >= COARSE_DEPTH + hx).astype(jnp.int32)
-
-    def coarse_first(i, carry):
-        w = coarse_weights[coarse_region(i), lax.rem(i + COARSE_DEPTH, 2)]
-        corr[i, pl.ds(8, coarse_work), :] = jnp.where(w > 0.5, coarse[i, pl.ds(8, coarse_work), :] * (1.0 / 6.0), 0.0)
-        return carry
-
-    lax.fori_loop(0, planes, coarse_first, 0)
+    def coarse_mask(at, parity):
+        return coarse_weights[region_of(at, COARSE_DEPTH, hx), parity % 2] > 0.5
+
+    def coarse_first(i, size, low):
+        for k in range(size):
+            start_value = coarse[i + k, pl.ds(8, coarse_work), :] * (1.0 / 6.0)
+            mask = coarse_mask(i + k, low + k + COARSE_DEPTH)
+            corr[i + k, pl.ds(8, coarse_work), :] = jnp.where(mask, start_value, 0.0)
+
+    in_groups(0, planes, GROUP, coarse_first)
     for t in range(1, 2 * COARSE):
-        def coarse_one(i, carry):
-            w = coarse_weights[coarse_region(i), lax.rem(i + COARSE_DEPTH + t, 2)]
-            centre, nbr = around(corr, i, 8, coarse_work, 2)
-            update = (coarse[i, pl.ds(8, coarse_work), :] + nbr) * (1.0 / 6.0)
-            corr[i, pl.ds(8, coarse_work), :] = jnp.where(w > 0.5, update, centre)
-            return carry
-
-        lax.fori_loop(t, planes - t, coarse_one, 0)
+        def coarse_one(i, size, low):
+            centres, sums = stencil(corr, i, size, 8, coarse_work, 2)
+            fresh = []
+            for k in range(size):
+                update = (coarse[i + k, pl.ds(8, coarse_work), :] + sums[k]) * (1.0 / 6.0)
+                fresh.append(jnp.where(coarse_mask(i + k, low + k + COARSE_DEPTH + t), update, centres[k]))
+            for k in range(size):
+                corr[i + k, pl.ds(8, coarse_work), :] = fresh[k]
+
+        in_groups(t, planes - t, GROUP, coarse_one)
 
     arrive(second_fine)
     sent(second_fine)
@@ -304,36 +377,34 @@
     half_rows = hy + 8
     first_plane = 2 * COARSE - 1
 
-    def add_correction(c, carry):
-        plane = corr[c, pl.ds(COARSE_ROW0 - 4, half_rows), :]
-        wide_rows[c, pl.ds(0, half_rows, stride=2), :] = plane
-        wide_rows[c, pl.ds(1, half_rows, stride=2), :] = plane
-        wide = wide_rows[c]
-        for b in range(2):
-            i = 2 * (c - COARSE_DEPTH) + DEPTH + b
-            post[i, pl.ds(ROW0 - 8, cy + 16), :] = post[i, pl.ds(ROW0 - 8, cy + 16), :] + wide
-        return carry
-
-    def add_end(c, b):
-        plane = corr[c, pl.ds(COARSE_ROW0 - 4, half_rows), :]
-        wide_rows[c, pl.ds(0, half_rows, stride=2), :] = plane
-        wide_rows[c, pl.ds(1, half_rows, stride=2), :] = plane
-        i = 2 * (c - COARSE_DEPTH) + DEPTH + b
-        post[i, pl.ds(ROW0 - 8, cy + 16), :] = post[i, pl.ds(ROW0 - 8, cy + 16), :] + wide_rows[c]
-
-    add_end(first_plane, 1)
-    lax.fori_loop(first_plane + 1, planes - first_plane - 1, add_correction, 0)
-    add_end(planes - first_plane - 1, 0)
+    def add_correction(c, size, low, sides=(0, 1)):
+        for k in range(size):
+            plane = corr[c + k, pl.ds(COARSE_ROW0 - 4, half_rows), :]
+            wide_rows[c + k, pl.ds(0, half_rows, stride=2), :] = plane
+            wide_rows[c + k, pl.ds(1, half_rows, stride=2), :] = plane
+        rows = pl.ds(ROW0 - 8, cy + 16)
+        fresh = []
+        for k in range(size):
+            wide = wide_rows[c + k]
+            for b in sides:
+                i = 2 * (c + k - COARSE_DEPTH) + DEPTH + b
+                fresh.append((i, post[i, rows, :] + wide))
+        for i, value in fresh:
+            post[i, rows, :] = value
+
+    add_correction(first_plane, 1, 0, (1,))
+    in_groups(first_plane + 1, planes - first_plane - 1, 2, add_correction)
+    add_correction(planes - first_plane - 1, 1, 0, (0,))
 
     smooth(post, POST)
     store_smoothed = pltpu.make_async_copy(post.at[own_planes, own_rows], smoothed_ref, local_sem.at[0])
     store_smoothed.start()
 
-    def last(i, carry):
-        res_rows[i] = defect(post, DEPTH + i)[1]
-        return carry
-
-    lax.fori_loop(0, cx, last, 0)
+    def last(i, size, low):
+        for k, value in enumerate(defects(post, DEPTH + i, size)[1]):
+            res_rows[i + k] = value
+
+    in_groups(0, cx, GROUP, last)
     store_residual = pltpu.make_async_copy(res_rows, residual_ref, local_sem.at[1])
     store_residual.start()
     for c in msum + gsum:
@@ -362,6 +433,7 @@
             pltpu.VMEM(wide, f32),
             pltpu.VMEM(narrow, f32),
             pltpu.VMEM(narrow, f32),
+            pltpu.VMEM((3, 2 * (hx // 2), COARSE_DEPTH, cz), f32),
             pltpu.VMEM((3, 3, 8, cz), f32),
             pltpu.VMEM((3, 2, cy + 2 * SWEEP_DEPTH, cz), f32),
             pltpu.VMEM((3, 2, hy + 16, cz), f32),
@@ -371,8 +443,8 @@
             pltpu.VMEM((members, 8, cz), f32),
             pltpu.VMEM((groups, 8, cz), f32),
             dma((2,)),
-            dma((5, len(SIDES))),
-            dma((5, len(SIDES))),
+            dma((1 + 4 * STEPS, len(SIDES))),
+            dma((1 + 4 * STEPS, len(SIDES))),
             dma((members,)),
             dma((members,)),
             dma((groups,)),

time: 63.8 us -> 39.5 us (0.62)
  Pallas kernels: 60.3 us -> 35.9 us
    pallas_call x1, Pallas kernels: 60.3 us -> 35.9 us  [per_device(): pl.pallas_call(functools.partial(kernel, dims, (cx, cy, cz)), out_shape=[...]
where the time goes in v2:
time: 39.5 us; the launch traced here: 39.3 us
  Pallas kernels  35.9 us (91%)
  local copies, waits for them, and re-layouts  2.72 us (7%)
  between operations  0.65 us (2%)
    pallas_call x1, Pallas kernels, per_device(): pl.pallas_call(functools.partial(kernel, dims, (cx, cy, cz)), out_shape=[...  35.9 us
    unnamed x4, local copies, waits for them, and re-layouts  2.72 us

profile of v2, /device:TPU:0, one launch (start us, length us, event | category | flops | bytes accessed | tf_op | source)
XLA Modules:
  0.0 39.3 jit_solution(7351527892868052694)
XLA Ops:
  0.6 35.9 %shard_map.50 = (f32[32,32,128]{2,1,0:T(8,128)}, f32[32,32,128]{2,1,0:T(8,128)}) custom-call(s32[1,1,4]{2,1,0:T(1,128)} %refined_ref.1, f32[32,32,128]{2,1,0:T(8,128)} %source_ref.1, f32[32,32,128]{2,1,0:T(8,128)} %potential_ref.1), custom_call_target="tpu_custom_call" | custom-call | tf_op jit(solution)/shard_map/pallas_call | solution.py:425
  36.6 0.0 copy-start
  36.6 1.9 %copy.7 = f32[32,32,128]{2,1,0:T(8,128)} copy(f32[32,32,128]{2,1,0:T(8,128)} %get-tuple-element.4) | data formatting | bytes 1048576
  38.5 0.0 copy-done
  38.5 0.8 %copy.8 = f32[32,32,128]{2,1,0:T(8,128)} copy(f32[32,32,128]{2,1,0:T(8,128)S(1)} %copy-done) | data formatting | bytes 1048576
Async XLA Ops:
  36.6 1.9 %copy-start = (f32[32,32,128]{2,1,0:T(8,128)S(1)}, f32[32,32,128]{2,1,0:T(8,128)}, u32[]{:S(2)}) copy-start(f32[32,32,128]{2,1,0:T(8,128)} %get-tuple-element.5) | copy-start | bytes 1572868

commit v3 on v2

--- a/solution.py
+++ b/solution.py
@@ -69,7 +69,9 @@
 
     load_rhs = pltpu.make_async_copy(source_ref, rhs.at[own_planes, own_rows], local_sem.at[0])
     load_fine = pltpu.make_async_copy(potential_ref, fine.at[own_planes, own_rows], local_sem.at[1])
+    load_sent = pltpu.make_async_copy(potential_ref, res_rows, local_sem.at[2])
     load_rhs.start()
+    load_sent.start()
     load_fine.start()
 
     def there(dx, dy):
@@ -143,6 +145,7 @@
         return acc
 
     member_sums[0] = lax.fori_loop(0, cx, add_plane, jnp.zeros((8, cz), jnp.float32))
+    load_sent.wait()
     load_fine.wait()
     pl.semaphore_wait(barrier, expected)
 
@@ -160,13 +163,16 @@
     for c in msum:
         c.start()
 
-    def halo_copies(kind, n, src, dst, counts, offsets, depth, skip=0):
+    def halo_copies(kind, n, src, dst, counts, offsets, depth, skip=0, base=None):
         dx, dy = SIDES[n]
         steps = corner_steps(depth) if dx and dy else [(skip, depth, depth)]
         copies = []
         for m, (begin, end, reach) in enumerate(steps):
             sx, tx = slabs(dx, counts[0], offsets[0], begin, end)
             sy, ty = slabs(dy, counts[1], offsets[1], 0 if dx else skip, reach)
+            if base is not None:
+                sx = pl.ds(sx.start - offsets[0] + base, sx.size)
+                sy = pl.ds(sy.start - offsets[1] + base, sy.size)
             copies.append(pltpu.make_async_remote_copy(
                 src_ref=src.at[sx, sy], dst_ref=dst.at[tx, ty],
                 send_sem=send_sem.at[kind + m, n], recv_sem=recv_sem.at[kind + m, n],
@@ -183,7 +189,7 @@
                 device_id=device(dx, dy), device_id_type=MESH,
             ),
         ] + (
-            halo_copies(1, n, fine, fine, (cx, cy), (DEPTH, ROW0), DEPTH)
+            halo_copies(1, n, res_rows, fine, (cx, cy), (DEPTH, ROW0), DEPTH, 0, 0)
             + halo_copies(1 + STEPS, n, rhs, rhs, (cx, cy), (DEPTH, ROW0), SWEEP_DEPTH)
         )
 
@@ -209,8 +215,11 @@
                 for c in round_of(n):
                     c.start()
 
-    def arrive(round_of):
+    def arrive(round_of, sides=SIDES):
         for n, (dx, dy) in enumerate(SIDES):
+            if (dx, dy) not in sides:
+                continue
+
             @pl.when(there(-dx, -dy))
             def _():
                 for c in round_of(n):
@@ -240,18 +249,19 @@
         total = total + group_sums[o]
     mean = jnp.sum(total) / (cx * cy * cz * groups * members)
 
-    arrive(first_round)
-    sent(first_round)
-
-    frow = lax.broadcasted_iota(jnp.int32, (work, cz), 0) - SWEEP_DEPTH
-    flane = lax.broadcasted_iota(jnp.int32, (work, cz), 1)
-    fbase = (frow + flane) & 1
-    for region in range(3):
-        here = jnp.where(
-            frow < 0, flags[region, 0, 0:1, :], jnp.where(frow < cy, flags[region, 1, 0:1, :], flags[region, 2, 0:1, :])
-        )
-        for q in range(2):
-            weights[region, q] = jnp.where(fbase == q, here, 0.0)
+    along = ((-1, 0), (1, 0))
+    arrive(first_round, along)
+
+    def fine_masks(row, rows, member):
+        frow = lax.broadcasted_iota(jnp.int32, (rows, cz), 0) + row
+        flane = lax.broadcasted_iota(jnp.int32, (rows, cz), 1)
+        fbase = (frow + flane) & 1
+        for region in range(3):
+            here = flags[region, member, 0:1, :]
+            for q in range(2):
+                weights[region, q, pl.ds(SWEEP_DEPTH + row, rows), :] = jnp.where(fbase == q, here, 0.0)
+
+    fine_masks(0, cy, 1)
 
     def lanes(value, step):
         lane = lax.broadcasted_iota(jnp.int32, value.shape, 1)
@@ -279,24 +289,40 @@
         if (high - low) % size:
             one(low + whole * size, (high - low) % size, low)
 
-    def smooth(field, count):
+    def smooth(field, count, bands):
         for t in range(2 * count):
             reach = 2 * count - t
 
             def one(i, size, low):
-                centres, sums = stencil(field, i, size, 8, work, 1)
-                fresh = []
-                for k in range(size):
-                    at = i + k
-                    mask = weights[region_of(at, DEPTH, cx), (low + k + DEPTH + t) % 2] > 0.5
-                    update = (rhs[at, pl.ds(8, work), :] - mean + sums[k]) * (1.0 / 6.0)
-                    fresh.append(jnp.where(mask, update, centres[k]))
-                for k in range(size):
-                    field[i + k, pl.ds(8, work), :] = fresh[k]
+                stores = []
+                for row, rows, limit in bands:
+                    centres, sums = stencil(field, i, size, row, rows, 1)
+                    allowed = limit(t)
+                    for k in range(size):
+                        at = i + k
+                        region = region_of(at, DEPTH, cx)
+                        parity = (low + k + DEPTH + t) % 2
+                        mask = weights[region, parity, pl.ds(row - 8, rows), :] > 0.5
+                        if allowed is not None:
+                            mask = mask & allowed
+                        update = (rhs[at, pl.ds(row, rows), :] - mean + sums[k]) * (1.0 / 6.0)
+                        stores.append((at, row, rows, jnp.where(mask, update, centres[k])))
+                for at, row, rows, value in stores:
+                    field[at, pl.ds(row, rows), :] = value
 
             in_groups(DEPTH - reach, DEPTH + cx + reach, GROUP, one)
 
-    smooth(fine, PRE)
+    edge = 2 * SWEEP_DEPTH
+    inner_row = lax.broadcasted_iota(jnp.int32, (cy - 2, cz), 0) + 1
+    edge_row = lax.broadcasted_iota(jnp.int32, (edge, cz), 0) - SWEEP_DEPTH
+    smooth(fine, PRE, [(ROW0 + 1, cy - 2, lambda t: (inner_row > t) & (inner_row < cy - 1 - t))])
+    arrive(first_round, [side for side in SIDES if side not in along])
+    fine_masks(-SWEEP_DEPTH, SWEEP_DEPTH, 0)
+    fine_masks(cy, SWEEP_DEPTH, 2)
+    smooth(fine, PRE, [
+        (ROW0 - SWEEP_DEPTH, edge, lambda t: edge_row <= t),
+        (ROW0 + cy - SWEEP_DEPTH, edge, lambda t: edge_row >= -1 - t),
+    ])
 
     lane = lax.broadcasted_iota(jnp.int32, (cy, cz), 1)
     even = lane % 2 == 0
@@ -396,9 +422,10 @@
     in_groups(first_plane + 1, planes - first_plane - 1, 2, add_correction)
     add_correction(planes - first_plane - 1, 1, 0, (0,))
 
-    smooth(post, POST)
+    smooth(post, POST, [(8, work, lambda t: None)])
     store_smoothed = pltpu.make_async_copy(post.at[own_planes, own_rows], smoothed_ref, local_sem.at[0])
     store_smoothed.start()
+    sent(first_round)
 
     def last(i, size, low):
         for k, value in enumerate(defects(post, DEPTH + i, size)[1]):
@@ -442,7 +469,7 @@
             pltpu.VMEM((cx, cy, cz), f32),
             pltpu.VMEM((members, 8, cz), f32),
             pltpu.VMEM((groups, 8, cz), f32),
-            dma((2,)),
+            dma((3,)),
             dma((1 + 4 * STEPS, len(SIDES))),
             dma((1 + 4 * STEPS, len(SIDES))),
             dma((members,)),

time: 39.5 us -> 38.2 us (0.967)
  Pallas kernels: 35.9 us -> 34.7 us
    pallas_call x1, Pallas kernels: 35.9 us -> 34.7 us  [per_device(): pl.pallas_call(functools.partial(kernel, dims, (cx, cy, cz)), out_shape=[...]
where the time goes in v3:
time: 38.2 us; the launch traced here: 38.1 us
  Pallas kernels  34.7 us (91%)
  local copies, waits for them, and re-layouts  2.72 us (7%)
  between operations  0.65 us (2%)
    pallas_call x1, Pallas kernels, per_device(): pl.pallas_call(functools.partial(kernel, dims, (cx, cy, cz)), out_shape=[...  34.7 us
    unnamed x4, local copies, waits for them, and re-layouts  2.72 us

profile of v3, /device:TPU:0, one launch (start us, length us, event | category | flops | bytes accessed | tf_op | source)
XLA Modules:
  0.0 38.1 jit_solution(16999064785891589469)
XLA Ops:
  0.6 34.7 %shard_map.50 = (f32[32,32,128]{2,1,0:T(8,128)}, f32[32,32,128]{2,1,0:T(8,128)}) custom-call(s32[1,1,4]{2,1,0:T(1,128)} %refined_ref.1, f32[32,32,128]{2,1,0:T(8,128)} %source_ref.1, f32[32,32,128]{2,1,0:T(8,128)} %potential_ref.1), custom_call_target="tpu_custom_call" | custom-call | tf_op jit(solution)/shard_map/pallas_call | solution.py:452
  35.3 0.0 copy-start
  35.3 1.9 %copy.7 = f32[32,32,128]{2,1,0:T(8,128)} copy(f32[32,32,128]{2,1,0:T(8,128)} %get-tuple-element.4) | data formatting | bytes 1048576
  37.3 0.0 copy-done
  37.3 0.8 %copy.8 = f32[32,32,128]{2,1,0:T(8,128)} copy(f32[32,32,128]{2,1,0:T(8,128)S(1)} %copy-done) | data formatting | bytes 1048576
Async XLA Ops:
  35.3 1.9 %copy-start = (f32[32,32,128]{2,1,0:T(8,128)S(1)}, f32[32,32,128]{2,1,0:T(8,128)}, u32[]{:S(2)}) copy-start(f32[32,32,128]{2,1,0:T(8,128)} %get-tuple-element.5) | copy-start | bytes 1572868
